TPU v7x, 32 devices: a 4x4x1 block of a 4x4x8 slice. The times are simulated.
32 devices in a mesh: layer: 1 (over z), tensor: 32 (over y, x, core).
Axes of the slice: x: 4, y: 4, z: 1, core: 2. Of those that a mesh axis runs over, the one named last changes fastest.
The devices are a block of a 4x4x8 slice.
Arguments:
- gradient: bfloat16 [4096, 4096], P('layer', 'tensor')
- left_stat: float32 [4096, 4096], P('layer')
- right_stat: float32 [4096, 1024], P(('layer', 'tensor'))
- left_root: bfloat16 [4096, 4096], P('layer')
- right_root: bfloat16 [4096, 1024], P(('layer', 'tensor'))
Outputs:
- output 1: float32 [4096, 4096], P('layer')
- output 2: float32 [4096, 1024], P(('layer', 'tensor'))
- output 3: float32 [4096, 4096], P('layer', 'tensor')
All inputs are finite; a program needn't handle non-finite values.
Results may differ from a plain program's by a relative error of at most 0.001.
Values are sent between devices in bfloat16 or wider.
A program may use at most 768 MiB of HBM per device.

v0:
```python
import jax
import jax.numpy as jnp
from jax import lax
from jax.sharding import PartitionSpec as P

EMA_DECAY = 0.9


def group_gather(shard, tensor_size, group_size):
    my_index = lax.axis_index('tensor')
    gathered = shard
    distance = 1
    while distance < group_size:
        perm_pairs = [(source, source ^ distance) for source in range(tensor_size)]
        partner = lax.ppermute(gathered, 'tensor', perm_pairs)
        is_upper = (my_index // distance) % 2 == 1
        low_half = jnp.where(is_upper, partner, gathered)
        high_half = jnp.where(is_upper, gathered, partner)
        gathered = jnp.concatenate([low_half, high_half], axis=1)
        distance = distance * 2
    return gathered


def solution(mesh):
    tensor_size = mesh.shape['tensor']
    stat_spec = P('layer', None)
    shard_spec = P('layer', 'tensor')
    row_spec = P(('layer', 'tensor'), None)

    def local_step(gradient, left_stat, right_stat, left_root, right_root):
        shard_cols = gradient.shape[1]
        block_size = right_stat.shape[1]
        group_size = block_size // shard_cols
        left_part = jnp.einsum('mw,kw->mk', gradient, gradient, preferred_element_type=jnp.float32)
        left_sum = lax.psum(left_part, 'tensor')
        group_grad = group_gather(gradient, tensor_size, group_size)
        right_prod = jnp.einsum('mw,mb->wb', gradient, group_grad, preferred_element_type=jnp.float32)
        precond = jnp.einsum('mb,wb->mw', group_grad, right_root, preferred_element_type=jnp.float32).astype(jnp.bfloat16)
        direction = jnp.dot(left_root, precond, preferred_element_type=jnp.float32)
        left_new = EMA_DECAY * left_stat + (1.0 - EMA_DECAY) * left_sum
        right_new = EMA_DECAY * right_stat + (1.0 - EMA_DECAY) * right_prod
        return left_new, right_new, direction

    return jax.shard_map(local_step, mesh=mesh, in_specs=(shard_spec, stat_spec, row_spec, stat_spec, row_spec), out_specs=(stat_spec, row_spec, shard_spec), check_vma=False)
```

profile of v0, /device:TPU:97, one launch (start us, length us, event | category | flops | bytes accessed | tf_op | source)
XLA Modules:
  0.0 680.7 jit_solution(9017324894257766468)
XLA Ops:
  7.2 0.0 copy-start
  7.2 0.1 all-reduce.2.cloned.1.call-start
  7.3 26.6 %fusion.9 = f32[4096,4096]{1,0:T(8,128)} fusion(bf16[4096,128]{1,0:T(8,128)(2,1)} %param.5), kind=kOutput, calls=%fused_computation.19 | convolution fusion | flops 4294967296 | bytes 68157440 | tf_op jit(solution)/shard_map/mw,kw->mk/dot_general | solution.py:34
  33.9 0.0 copy-start.3
  33.9 0.1 all-reduce.2.cloned.1.call-update
  33.9 1.2 copy-done.3
  35.1 2.0 collective-permute-start
  37.1 2.3 collective-permute-done
  39.4 0.1 broadcast_select_fusion.5
  39.5 0.0 copy-start.4
  39.5 0.0 copy-start.5
  39.6 1.0 copy-done.4
  40.5 0.2 pad_maximum_fusion.8
  40.8 0.1 copy-done.5
  40.9 0.8 collective-permute-start.1
  41.6 67.0 %collective-permute-done.1 = bf16[4096,256]{1,0:T(8,128)(2,1)} collective-permute-done((bf16[4096,256]{1,0:T(8,128)(2,1)S(1)}, bf16[4096,256]{1,0:T(8,128)(2,1)}, u32[]{:S(2)}, u32[]{:S(2)}) %collective-permute-start.1) | collective-permute-done | bytes 2097184 | tf_op jit(solution)/shard_map/ppermute | solution.py:15
  108.6 3.0 broadcast_select_fusion.3
  111.6 0.0 copy-start.2
  111.7 2.6 pad_maximum_fusion.5
  114.2 0.1 copy-done.2
  114.3 2.5 collective-permute-start.2
  116.8 2.0 copy.8
  118.9 0.0 copy-start.8
  118.9 133.6 %collective-permute-done.2 = bf16[4096,512]{1,0:T(8,128)(2,1)} collective-permute-done((bf16[4096,512]{1,0:T(8,128)(2,1)}, bf16[4096,512]{1,0:T(8,128)(2,1)}, u32[]{:S(2)}, u32[]{:S(2)}) %collective-permute-start.2) | collective-permute-done | bytes 4194336 | tf_op jit(solution)/shard_map/ppermute | solution.py:15
  252.5 3.7 broadcast_select_fusion.1
  256.2 0.0 copy-start.6
  256.2 0.0 copy-start.7
  256.2 2.0 copy-done.6
  258.2 1.4 copy-done.7
  259.6 0.0 copy-done.8
  259.6 2.4 fusion.5
  261.9 1.0 copy.9
  262.9 0.0 copy-done
  262.9 22.8 %convolution_bitcast_fusion = f32[4096,128]{0,1:T(8,128)S(1)} fusion(bf16[4096,4096]{1,0:T(8,128)(2,1)} %param.8, bf16[128,1024]{1,0:T(8,128)(2,1)S(1)} %copy-done, bf16[4096,512]{1,0:T(8,128)(2,1)} %copy-done.7, bf16[4096,512]{1,0:T(8,128)(2,1)} %copy-done.6), kind=kOutput, calls=%fused_computation.4 | convolution fusion | flops 5386010624 | bytes 44302336 | tf_op jit(solution)/shard_map/dot_general | solution.py:39
  285.8 1.8 copy.10
  287.6 321.8 %all-reduce.2.cloned.1.call-done = f32[4096,4096]{1,0:T(8,128)} async-done(((f32[4096,4096]{1,0:T(8,128)}), f32[4096,4096]{1,0:T(8,128)}) %all-reduce.2.cloned.1.call-update) | async-done | bytes 67108880 | tf_op jit(solution)/shard_map/psum | solution.py:35
  609.4 0.0 copy-start.1
  609.4 64.3 %multiply_add_fusion = f32[4096,4096]{1,0:T(8,128)} fusion(f32[4096,4096]{1,0:T(8,128)} %all-reduce.2.cloned.1.call-done, f32[4096,4096]{1,0:T(8,128)} %param.6), kind=kLoop, calls=%fused_computation | loop fusion | flops 50331648 | bytes 201326592 | tf_op jit(solution)/shard_map/add | solution.py:40
  673.8 0.0 copy-done.1
Async XLA Ops:
  7.2 255.8 %copy-start = (bf16[128,1024]{1,0:T(8,128)(2,1)S(1)}, bf16[128,1024]{1,0:T(8,128)(2,1)}, u32[]{:S(2)}) copy-start(bf16[128,1024]{1,0:T(8,128)(2,1)} %param.9) | copy-start | bytes 786436
  7.2 602.2 %all-reduce.2.cloned.1.call-start = ((), (), s32[]{:S(2)}) async-start(), calls=%async_computation | async-start | bytes 134217728 | tf_op jit(solution)/shard_map/psum | solution.py:35
  33.9 1.2 copy-start.3
  35.1 4.3 collective-permute-start
  39.5 1.0 copy-start.4
  39.5 1.3 copy-start.5
  40.9 67.8 %collective-permute-start.1 = (bf16[4096,256]{1,0:T(8,128)(2,1)S(1)}, bf16[4096,256]{1,0:T(8,128)(2,1)}, u32[]{:S(2)}, u32[]{:S(2)}) collective-permute-start(bf16[4096,256]{1,0:T(8,128)(2,1)S(1)} %pad_maximum_fusion.8), channel_id=1, source_target_pairs={{0,2},{1,3},{2,0},{3,1},{4,6},{5,7},{6,4},{7,5},{8,10},{9,11},{10,... | collective-permute-start | bytes 6291464 | tf_op jit(solution)/shard_map/ppermute | solution.py:15
  111.6 2.7 copy-start.2
  114.3 138.2 %collective-permute-start.2 = (bf16[4096,512]{1,0:T(8,128)(2,1)}, bf16[4096,512]{1,0:T(8,128)(2,1)}, u32[]{:S(2)}, u32[]{:S(2)}) collective-permute-start(bf16[4096,512]{1,0:T(8,128)(2,1)} %pad_maximum_fusion.5), channel_id=1, source_target_pairs={{0,4},{1,5},{2,6},{3,7},{4,0},{5,1},{6,2},{7,3},{8,12},{9,13},{10,... | collective-permute-start | bytes 12582920 | tf_op jit(solution)/shard_map/ppermute | solution.py:15
  118.9 140.7 %copy-start.8 = (f32[128,1024]{0,1:T(8,128)S(1)}, f32[128,1024]{0,1:T(8,128)}, u32[]{:S(2)}) copy-start(f32[128,1024]{0,1:T(8,128)} %copy.8) | copy-start | bytes 1572868
  256.2 2.0 copy-start.6
  256.2 3.4 copy-start.7
  609.4 64.3 %copy-start.1 = (bf16[128,1024]{1,0:T(8,128)(2,1)S(1)}, bf16[128,1024]{1,0:T(8,128)(2,1)}, u32[]{:S(2)}) copy-start(bf16[128,1024]{1,0:T(8,128)(2,1)} %param.9) | copy-start | bytes 786436
Sparse Core Ops, SparseCore 0:
  34.0 575.3 all-reduce.1
where the time goes:
time: 681 us
  waiting for transfers between devices  525 us (77%)
  other arithmetic  74 us (11%)
  matrix products  51.8 us (8%)
  between operations  14.2 us (2%)
  local copies, waits for them, and re-layouts  10.6 us (2%)
    psum x1, waiting for transfers between devices, local_step(): left_sum = lax.psum(left_part, 'tensor')  322 us
    ppermute x3, waiting for transfers between devices, group_gather(): partner = lax.ppermute(gathered, 'tensor', perm_pairs)  203 us
    add x1, other arithmetic, local_step(): left_new = EMA_DECAY * left_stat + (1.0 - EMA_DECAY) * left_sum  64.3 us
    dot_general x1, matrix products, local_step(): jnp.einsum('mw,kw->mk', gradient, gradient, preferred_element_type=jnp.fl...  26.6 us
    dot_general x1, matrix products, local_step(): direction = jnp.dot(left_root, precond, preferred_element_type=jnp.float32)  22.8 us
  transfers between devices with their start and end apart: 4, of which 4 were waited for; matrix products, arithmetic and copies ran while one was open for 6% of the time, Pallas kernels for 0%

commit v1 on v0

v1 whole, which is shorter than its diff:
```python
import functools

import jax
import jax.numpy as jnp
from jax import lax
from jax.experimental import pallas as pl
from jax.experimental.pallas import tpu as pltpu
from jax.sharding import PartitionSpec as P


EMA_DECAY = 0.9
ROW_PARTS = (2, 2, 2, 1, 1)
TILE = 256
SLABS_PER_DOT = 8
NT = (((1,), (1,)), ((), ()))
TN = (((0,), (0,)), ((), ()))
ANY = pl.BlockSpec(memory_space=pltpu.HBM)


def left_kernel(index, sizes, aliased, *refs):
    chunk_refs = refs[: index + 1]
    refs = refs[index + 1:]
    left_ref = refs[0]
    out_ref = refs[2 if aliased else 1]
    rows_buf, cols_buf, acc, left_a, left_b, out_a, out_b, row_sem, col_sem, la_sem, lb_sem, oa_sem, ob_sem = refs[
        3 if aliased else 2:]
    height = sizes[index]
    base = sum(sizes[:index])
    n_slabs = rows_buf.shape[0]
    n_off = base // TILE
    n_diag = height // TILE
    total = n_off + n_diag

    def load_rows():
        return pltpu.make_async_copy(chunk_refs[index], rows_buf, row_sem)

    def col_copy(k, start, slot):
        return pltpu.make_async_copy(chunk_refs[k].at[:, pl.ds(start, TILE), :], cols_buf.at[slot], col_sem.at[slot])

    def a_in(tile, slot):
        return pltpu.make_async_copy(
            left_ref.at[pl.ds(base, height), pl.ds(pl.multiple_of(tile * TILE, TILE), TILE)], left_a.at[slot], la_sem.at[slot])

    def b_in(tile, slot):
        return pltpu.make_async_copy(
            left_ref.at[pl.ds(pl.multiple_of(tile * TILE, TILE), TILE), pl.ds(base, height)], left_b.at[slot], lb_sem.at[slot])

    def a_out(tile, slot):
        return pltpu.make_async_copy(
            out_a.at[slot], out_ref.at[pl.ds(base, height), pl.ds(pl.multiple_of(tile * TILE, TILE), TILE)], oa_sem.at[slot])

    def b_out(tile, slot):
        return pltpu.make_async_copy(
            out_b.at[slot], out_ref.at[pl.ds(pl.multiple_of(tile * TILE, TILE), TILE), pl.ds(base, height)], ob_sem.at[slot])

    def fetch(step, slot):
        @pl.when(step < n_diag)
        def _():
            a_in(n_off + step, slot).start()

        if n_off:
            @pl.when(step >= n_diag)
            def _():
                tile = step - n_diag
                a_in(tile, slot).start()
                b_in(tile, slot).start()
                first = 0
                for k in range(index):
                    count = sizes[k] // TILE

                    @pl.when(jnp.logical_and(tile >= first, tile < first + count))
                    def _(k=k, first=first):
                        col_copy(k, pl.multiple_of((tile - first) * TILE, TILE), slot).start()

                    first += count

    def product(load_cols):
        def piece(kk, _):
            lhs = jnp.concatenate([rows_buf[kk * SLABS_PER_DOT + j] for j in range(SLABS_PER_DOT)], axis=1)
            rhs = jnp.concatenate([load_cols(kk * SLABS_PER_DOT + j) for j in range(SLABS_PER_DOT)], axis=1)
            part = lax.dot_general(lhs, rhs, NT, preferred_element_type=jnp.float32)

            @pl.when(kk == 0)
            def _():
                acc[...] = part

            @pl.when(kk > 0)
            def _():
                acc[...] = acc[...] + part

            return 0

        lax.fori_loop(0, n_slabs // SLABS_PER_DOT, piece, 0)

    load_rows().start()
    fetch(0, 0)
    load_rows().wait()

    def diag(step, _):
        slot = lax.rem(step, 2)
        a_in(0, slot).wait()

        @pl.when(step + 1 < total)
        def _():
            fetch(step + 1, 1 - slot)

        start = pl.multiple_of(step * TILE, TILE)
        product(lambda j: rows_buf[j, pl.ds(start, TILE), :])

        @pl.when(step >= 2)
        def _():
            a_out(0, slot).wait()

        out_a[slot] = EMA_DECAY * left_a[slot] + (1.0 - EMA_DECAY) * acc[...]
        a_out(n_off + step, slot).start()
        return 0

    lax.fori_loop(0, n_diag, diag, 0)

    if n_off:
        def off(tile, _):
            step = tile + n_diag
            slot = lax.rem(step, 2)
            a_in(0, slot).wait()
            b_in(0, slot).wait()
            col_copy(0, 0, slot).wait()

            @pl.when(step + 1 < total)
            def _():
                fetch(step + 1, 1 - slot)

            product(lambda j: cols_buf[slot, j])

            @pl.when(step >= 2)
            def _():
                a_out(0, slot).wait()

            @pl.when(tile >= 2)
            def _():
                b_out(0, slot).wait()

            out_a[slot] = EMA_DECAY * left_a[slot] + (1.0 - EMA_DECAY) * acc[...]
            out_b[slot] = EMA_DECAY * left_b[slot] + (1.0 - EMA_DECAY) * acc[...].T
            a_out(tile, slot).start()
            b_out(tile, slot).start()
            return 0

        lax.fori_loop(0, n_off, off, 0)
        for slot in range(min(n_off, 2)):
            b_out(0, slot).wait()
    for slot in range(min(total, 2)):
        a_out(0, slot).wait()


def left_update(index, sizes, chunks, left, partial_out):
    height = sizes[index]
    n_slabs, _, width = chunks[0].shape
    aliased = partial_out is not None
    operands = list(chunks) + [left] + ([partial_out] if aliased else [])
    done = sum(sizes[:index])
    area = height * height + 2 * height * done
    return pl.pallas_call(
        functools.partial(left_kernel, index, sizes, aliased),
        out_shape=jax.ShapeDtypeStruct(left.shape, left.dtype),
        in_specs=[ANY] * len(operands),
        out_specs=ANY,
        input_output_aliases={len(operands) - 1: 0} if aliased else {},
        scratch_shapes=[
            pltpu.VMEM((n_slabs, height, width), chunks[0].dtype),
            pltpu.VMEM((2, n_slabs, TILE, width), chunks[0].dtype),
            pltpu.VMEM((height, TILE), jnp.float32),
            pltpu.VMEM((2, height, TILE), jnp.float32),
            pltpu.VMEM((2, TILE, height), jnp.float32),
            pltpu.VMEM((2, height, TILE), jnp.float32),
            pltpu.VMEM((2, TILE, height), jnp.float32),
            pltpu.SemaphoreType.DMA,
        ] + [pltpu.SemaphoreType.DMA((2,))] * 5,
        compiler_params=pltpu.CompilerParams(vmem_limit_bytes=48 * 2**20),
        cost_estimate=pl.CostEstimate(
            flops=2 * n_slabs * width * height * (height + done), bytes_accessed=8 * area + 2 * n_slabs * width * (height + done),
            transcendentals=0),
        name="left_update",
    )(*operands)


def side_kernel(first, slabs_ref, own_ref, root_ref, left_root_ref, stat_ref, dir_in_ref, right_ref, dir_ref, precond):
    @pl.when(pl.program_id(0) == 0)
    def _():
        block = jnp.concatenate([slabs_ref[j] for j in range(slabs_ref.shape[0])], axis=1)
        precond[...] = lax.dot_general(block, root_ref[...], NT, preferred_element_type=jnp.float32).astype(precond.dtype)
        prod = lax.dot_general(own_ref[...], block, TN, preferred_element_type=jnp.float32)
        scale = EMA_DECAY if first else 1.0
        right_ref[...] = scale * stat_ref[...] + (1.0 - EMA_DECAY) * prod

    part = jnp.dot(left_root_ref[...], precond[...], preferred_element_type=jnp.float32)
    dir_ref[...] = part if first else dir_in_ref[...] + part


def side_update(index, sizes, group_slabs, own, root, left_root, stat, direction):
    height = sizes[index]
    rows, width = left_root.shape[0], own.shape[1]
    tile_m = rows // 8
    first = direction is None
    if first:
        direction = jnp.zeros((8, 128), jnp.float32)
        dir_spec = pl.BlockSpec((8, 128), lambda m: (0, 0))
    else:
        dir_spec = pl.BlockSpec((tile_m, width), lambda m: (m, 0))
    base = sum(sizes[:index])
    col_block = base // height
    return pl.pallas_call(
        functools.partial(side_kernel, first),
        grid=(rows // tile_m,),
        out_shape=(jax.ShapeDtypeStruct(stat.shape, jnp.float32), jax.ShapeDtypeStruct((rows, width), jnp.float32)),
        in_specs=[
            pl.BlockSpec(group_slabs.shape, lambda m: (0, 0, 0)),
            pl.BlockSpec((height, width), lambda m: (col_block, 0)),
            pl.BlockSpec(root.shape, lambda m: (0, 0)),
            pl.BlockSpec((tile_m, height), lambda m: (m, col_block)),
            pl.BlockSpec(stat.shape, lambda m: (0, 0)),
            dir_spec,
        ],
        out_specs=(pl.BlockSpec(stat.shape, lambda m: (0, 0)), pl.BlockSpec((tile_m, width), lambda m: (m, 0))),
        scratch_shapes=[pltpu.VMEM((height, width), own.dtype)],
        compiler_params=pltpu.CompilerParams(vmem_limit_bytes=32 * 2**20, dimension_semantics=("arbitrary",)),
        cost_estimate=pl.CostEstimate(flops=2 * rows * height * width, bytes_accessed=2 * rows * height, transcendentals=0),
        name="side_update",
    )(group_slabs, own, root, left_root, stat, direction)


def solution(mesh):
    stat_spec = P('layer', None)
    shard_spec = P('layer', 'tensor')
    row_spec = P(('layer', 'tensor'), None)

    def local_step(gradient, left_stat, right_stat, left_root, right_root):
        rows, width = gradient.shape
        group_size = right_stat.shape[1] // width
        group_start = lax.axis_index('tensor') // group_size * group_size
        unit = rows // sum(ROW_PARTS)
        sizes = tuple(part * unit for part in ROW_PARTS)
        chunks, base = [], 0
        for size in sizes:
            chunks.append(lax.all_gather(gradient[base:base + size], 'tensor', axis=0))
            base += size
        left_new, right_new, direction = None, right_stat, None
        for index in range(len(sizes)):
            left_new = left_update(index, sizes, chunks[:index + 1], left_stat, left_new)
            group_slabs = lax.dynamic_slice_in_dim(chunks[index], group_start, group_size, axis=0)
            right_new, direction = side_update(
                index, sizes, group_slabs, gradient, right_root, left_root, right_new, direction)
        return left_new, right_new, direction

    return jax.shard_map(local_step, mesh=mesh, in_specs=(shard_spec, stat_spec, row_spec, stat_spec, row_spec), out_specs=(stat_spec, row_spec, shard_spec), check_vma=False)
```

time: 681 us -> 430 us (0.63)
  waiting for transfers between devices: 525 us -> 183 us
  Pallas kernels: 0 us -> 220 us
  other arithmetic: 74 us -> 0 us
  matrix products: 51.8 us -> 0 us
    psum x1 -> x0, waiting for transfers between devices: 322 us -> none  [local_step(): left_sum = lax.psum(left_part, 'tensor')]
    pallas_call x0 -> x10, Pallas kernels: none -> 220 us  [the longest x5 181 us: left_update(): pl.pallas_call(functools.partial(left_kernel, index, sizes, aliased), out...]
    ppermute x3 -> x0, waiting for transfers between devices: 203 us -> none  [group_gather(): partner = lax.ppermute(gathered, 'tensor', perm_pairs)]
    all_gather x0 -> x5, waiting for transfers between devices: none -> 181 us  [local_step(): chunks.append(lax.all_gather(gradient[base:base + size], 'tensor', axis=0))]
    add x1 -> x0, other arithmetic: 64.3 us -> none  [local_step(): left_new = EMA_DECAY * left_stat + (1.0 - EMA_DECAY) * left_sum]
    dot_general x3 -> x0, matrix products: 51.8 us -> none  [the longest x1 26.6 us: local_step(): jnp.einsum('mw,kw->mk', gradient, gradient, preferred_element_type=jnp.fl...]
    unnamed x21 -> x12, local copies, waits for them, and re-layouts: 10.6 us -> 0.03 us
    dynamic_slice x0 -> x3, local copies, waits for them, and re-layouts: none -> 8.36 us  [local_step(): lax.dynamic_slice_in_dim(chunks[index], group_start, group_size, axis=0)]
  transfers between devices with their start and end apart: 4 -> 5, of which waited for: 4 -> 4; matrix products, arithmetic and copies ran while one was open for 6% -> 2% of each run, Pallas kernels for 0% -> 12%
where the time goes in v1:
time: 430 us
  Pallas kernels  220 us (51%)
  waiting for transfers between devices  183 us (43%)
  between operations  14 us (3%)
  local copies, waits for them, and re-layouts  12.1 us (3%)
    all_gather x5, waiting for transfers between devices, local_step(): chunks.append(lax.all_gather(gradient[base:base + size], 'tensor', axis=0))  181 us
    pallas_call x5, Pallas kernels, left_update(): pl.pallas_call(functools.partial(left_kernel, index, sizes, aliased), out...  181 us
    pallas_call x5, Pallas kernels, side_update(): pl.pallas_call(functools.partial(side_kernel, first), grid=(rows // tile_...  39.3 us
  transfers between devices with their start and end apart: 5, of which 4 were waited for; matrix products, arithmetic and copies ran while one was open for 2% of the time, Pallas kernels for 12%

profile of v1, /device:TPU:97, one launch (start us, length us, event | category | flops | bytes accessed | tf_op | source)
XLA Modules:
  0.0 429.5 jit_solution(14574644490841351372)
XLA Ops:
  7.2 0.1 all-gather.17.cloned.1.call-start
  7.2 1.7 fusion
  8.9 0.1 all-gather.17.cloned.1.call-update
  9.0 0.1 all-gather.19.cloned.1.call-start
  9.1 0.7 all-gather.19.cloned.1.call-update
  9.8 0.1 all-gather.11.cloned.1.call-start
  9.9 2.0 fusion.1
  11.9 0.1 all-gather.11.cloned.1.call-update
  11.9 0.1 all-gather.13.cloned.1.call-start
  12.0 0.6 all-gather.13.cloned.1.call-update
  12.6 0.1 all-gather.15.cloned.1.call-start
  12.6 0.6 all-gather.15.cloned.1.call-update
  13.2 42.1 %all-gather.17.cloned.1.call-done = bf16[16384,128]{1,0:T(8,128)(2,1)} async-done(((bf16[512,128]{1,0:T(8,128)(2,1)}), bf16[16384,128]{1,0:T(8,128)(2,1)}) %all-gather.17.cloned.1.call-update) | async-done | bytes 4194320 | tf_op jit(solution)/shard_map/all_gather | solution.py:244
  55.3 42.4 %all-gather.19.cloned.1.call-done = bf16[16384,128]{1,0:T(8,128)(2,1)} async-done(((bf16[512,128]{1,0:T(8,128)(2,1)}), bf16[16384,128]{1,0:T(8,128)(2,1)}) %all-gather.19.cloned.1.call-update) | async-done | bytes 4194320 | tf_op jit(solution)/shard_map/all_gather | solution.py:244
  97.7 2.7 constant_dynamic-slice_fusion.3
  100.4 47.0 %all-gather.11.cloned.1.call-done = bf16[32768,128]{1,0:T(8,128)(2,1)} async-done(((bf16[1024,128]{1,0:T(8,128)(2,1)}), bf16[32768,128]{1,0:T(8,128)(2,1)}) %all-gather.11.cloned.1.call-update) | async-done | bytes 8388624 | tf_op jit(solution)/shard_map/all_gather | solution.py:244
  147.4 49.7 %all-gather.13.cloned.1.call-done = bf16[32768,128]{1,0:T(8,128)(2,1)} async-done(((bf16[1024,128]{1,0:T(8,128)(2,1)}), bf16[32768,128]{1,0:T(8,128)(2,1)}) %all-gather.13.cloned.1.call-update) | async-done | bytes 8388624 | tf_op jit(solution)/shard_map/all_gather | solution.py:244
  197.1 3.9 constant_dynamic-slice_fusion
  201.0 18.7 %left_update.5.refs_3_ = f32[4096,4096]{1,0:T(8,128)} custom-call(bf16[32,1024,128]{2,1,0:T(8,128)(2,1)} %bitcast.9, f32[4096,4096]{1,0:T(8,128)} %refs_5_.1), custom_call_target="tpu_custom_call" | custom-call | flops 8589934592 | bytes 16777216 | tf_op jit(solution)/shard_map/left_update/pallas_call | solution.py:162
  219.8 34.7 %left_update.6.refs_4_ = f32[4096,4096]{1,0:T(8,128)} custom-call(bf16[32,1024,128]{2,1,0:T(8,128)(2,1)} %bitcast.10, bf16[32,1024,128]{2,1,0:T(8,128)(2,1)} %bitcast.15, f32[4096,4096]{1,0:T(8,128)} %refs_5_.1, f32[4096,4096]{1,0:T(8,128)} %left_update.5.refs_3_), custom_call_target="tpu_custom_call", output_to_operand_aliasing={{}: (3, {})} | custom-call | flops 17179869184 | bytes 41943040 | tf_op jit(solution)/shard_map/left_update/pallas_call | solution.py:162
  254.4 0.0 all-gather.15.cloned.1.call-done
  254.5 1.7 constant_dynamic-slice_fusion.2.slabs_ref
  256.2 0.0 copy-start.1
  256.2 50.4 %left_update.7.refs_5_ = f32[4096,4096]{1,0:T(8,128)} custom-call(bf16[32,1024,128]{2,1,0:T(8,128)(2,1)} %bitcast.11, bf16[32,1024,128]{2,1,0:T(8,128)(2,1)} %bitcast.16, bf16[32,1024,128]{2,1,0:T(8,128)(2,1)} %bitcast.20, f32[4096,4096]{1,0:T(8,128)} %refs_5_.1, f32[4096,4096]{1,0:T(8,128)} %left_update.6.refs_4_), custom_call_target="tpu_custom_call", output_to_operand_aliasing={{}: (4, {})} | custom-call | flops 25769803776 | bytes 67108864 | tf_op jit(solution)/shard_map/left_update/pallas_call | solution.py:162
  306.6 0.0 copy-done.1
  306.7 35.2 %left_update.8.refs_6_ = f32[4096,4096]{1,0:T(8,128)} custom-call(bf16[32,1024,128]{2,1,0:T(8,128)(2,1)} %bitcast.12, bf16[32,1024,128]{2,1,0:T(8,128)(2,1)} %bitcast.17, bf16[32,1024,128]{2,1,0:T(8,128)(2,1)} %bitcast.21, bf16[32,512,128]{2,1,0:T(8,128)(2,1)S(1)} %bitcast.6, f32[4096,4096]{1,0:T(8,128)} %refs_5_.1, ...), custom_call_target="tpu_custom_call", output_to_operand_aliasing={{}: (5, {})} | custom-call | flops 15032385536 | bytes 56623104 | tf_op jit(solution)/shard_map/left_update/pallas_call | solution.py:162
  341.9 0.0 copy-start
  341.9 0.0 copy-start.2
  341.9 0.0 copy-start.3
  341.9 0.0 copy-start.5
  341.9 41.6 %left_update.9 = f32[4096,4096]{1,0:T(8,128)} custom-call(bf16[32,1024,128]{2,1,0:T(8,128)(2,1)} %bitcast.13, bf16[32,1024,128]{2,1,0:T(8,128)(2,1)} %bitcast.18, bf16[32,1024,128]{2,1,0:T(8,128)(2,1)} %bitcast.22, bf16[32,512,128]{2,1,0:T(8,128)(2,1)S(1)} %bitcast.7, bf16[32,512,128]{2,1,0:T(8,128)(2,1)} %bitcast.24, ...), custom_call_target="tpu_custom_call", output_to_operand_aliasing={{}: (6, {})} | custom-call | flops 17179869184 | bytes 65011712 | tf_op jit(solution)/shard_map/left_update/pallas_call | solution.py:162
  383.6 0.0 copy-done
  383.6 0.0 copy-done.2
  383.6 0.0 copy-done.3
  383.6 0.0 copy-done.5
  383.6 8.3 %side_update.5 = (f32[128,1024]{1,0:T(8,128)S(1)}, f32[4096,128]{1,0:T(8,128)S(1)}) custom-call(bf16[8,1024,128]{2,1,0:T(8,128)(2,1)S(1)} %copy-done.2, bf16[4096,128]{1,0:T(8,128)(2,1)S(1)} %copy-done, bf16[128,1024]{1,0:T(8,128)(2,1)S(1)} %copy-done.3, bf16[4096,4096]{1,0:T(8,128)(2,1)} %left_root_ref.9, f32[128,1024]{1,0:T(8,128)S(1)} %copy-done.5, ...), custom_call_target="tpu_custom_call" | custom-call | flops 1073741824 | bytes 8388608 | tf_op jit(solution)/shard_map/side_update/pallas_call | solution.py:211
  392.0 8.4 %side_update.6 = (f32[128,1024]{1,0:T(8,128)S(1)}, f32[4096,128]{1,0:T(8,128)S(1)}) custom-call(bf16[8,1024,128]{2,1,0:T(8,128)(2,1)S(1)} %get-tuple-element.29.slabs_ref, bf16[4096,128]{1,0:T(8,128)(2,1)S(1)} %copy-done, bf16[128,1024]{1,0:T(8,128)(2,1)S(1)} %copy-done.3, bf16[4096,4096]{1,0:T(8,128)(2,1)} %left_root_ref.9, ...), custom_call_target="tpu_custom_call" | custom-call | flops 1073741824 | bytes 8388608 | tf_op jit(solution)/shard_map/side_update/pallas_call | solution.py:211
  400.4 0.0 copy-start.4
  400.4 8.5 %side_update.7 = (f32[128,1024]{1,0:T(8,128)S(1)}, f32[4096,128]{1,0:T(8,128)S(1)}) custom-call(bf16[8,1024,128]{2,1,0:T(8,128)(2,1)S(1)} %constant_dynamic-slice_fusion.2.slabs_ref, bf16[4096,128]{1,0:T(8,128)(2,1)S(1)} %copy-done, bf16[128,1024]{1,0:T(8,128)(2,1)S(1)} %copy-done.3, bf16[4096,4096]{1,0:T(8,128)(2,1)} %left_root_ref.9, ...), custom_call_target="tpu_custom_call" | custom-call | flops 1073741824 | bytes 8388608 | tf_op jit(solution)/shard_map/side_update/pallas_call | solution.py:211
  408.8 0.0 copy-done.4
  408.8 6.4 %side_update.8 = (f32[128,1024]{1,0:T(8,128)S(1)}, f32[4096,128]{1,0:T(8,128)S(1)}) custom-call(bf16[8,512,128]{2,1,0:T(8,128)(2,1)S(1)} %copy-done.4, bf16[4096,128]{1,0:T(8,128)(2,1)S(1)} %copy-done, bf16[128,1024]{1,0:T(8,128)(2,1)S(1)} %copy-done.3, bf16[4096,4096]{1,0:T(8,128)(2,1)} %left_root_ref.9, f32[128,1024]{1,0:T(8,128)S(1)} %get-tuple-element.17.stat_ref, ...), custom_call_target="tpu_custom_call" | custom-call | flops 536870912 | bytes 4194304 | tf_op jit(solution)/shard_map/side_update/pallas_call | solution.py:211
  415.2 7.7 %side_update.9 = (f32[128,1024]{1,0:T(8,128)}, f32[4096,128]{1,0:T(8,128)}) custom-call(bf16[8,512,128]{2,1,0:T(8,128)(2,1)S(1)} %get-tuple-element.31.slabs_ref, bf16[4096,128]{1,0:T(8,128)(2,1)S(1)} %copy-done, bf16[128,1024]{1,0:T(8,128)(2,1)S(1)} %copy-done.3, bf16[4096,4096]{1,0:T(8,128)(2,1)} %left_root_ref.9, ...), custom_call_target="tpu_custom_call" | custom-call | flops 536870912 | bytes 4194304 | tf_op jit(solution)/shard_map/side_update/pallas_call | solution.py:211
  (1 shorter events, 0.0 us)
Async XLA Ops:
  7.2 48.1 %all-gather.17.cloned.1.call-start = ((), (), s32[]{:S(2)}) async-start(), calls=%async_computation.3 | async-start | bytes 4325376 | tf_op jit(solution)/shard_map/all_gather | solution.py:244
  9.0 88.7 %all-gather.19.cloned.1.call-start = ((), (), s32[]{:S(2)}) async-start(), calls=%async_computation.4 | async-start | bytes 4325376 | tf_op jit(solution)/shard_map/all_gather | solution.py:244
  9.8 137.6 %all-gather.11.cloned.1.call-start = ((), (), s32[]{:S(2)}) async-start(), calls=%async_computation | async-start | bytes 8650752 | tf_op jit(solution)/shard_map/all_gather | solution.py:244
  11.9 185.2 %all-gather.13.cloned.1.call-start = ((), (), s32[]{:S(2)}) async-start(), calls=%async_computation.1 | async-start | bytes 8650752 | tf_op jit(solution)/shard_map/all_gather | solution.py:244
  12.6 241.9 %all-gather.15.cloned.1.call-start = ((), (), s32[]{:S(2)}) async-start(), calls=%async_computation.2 | async-start | bytes 8650752 | tf_op jit(solution)/shard_map/all_gather | solution.py:244
  256.2 50.4 %copy-start.1 = (bf16[16384,128]{1,0:T(8,128)(2,1)S(1)}, bf16[16384,128]{1,0:T(8,128)(2,1)}, u32[]{:S(2)}) copy-start(bf16[16384,128]{1,0:T(8,128)(2,1)} %all-gather.17.cloned.1.call-done) | copy-start | bytes 12582916
  341.9 41.7 %copy-start = (bf16[4096,128]{1,0:T(8,128)(2,1)S(1)}, bf16[4096,128]{1,0:T(8,128)(2,1)}, u32[]{:S(2)}) copy-start(bf16[4096,128]{1,0:T(8,128)(2,1)} %own_ref.9) | copy-start | bytes 3145732
  341.9 41.7 %copy-start.2 = (bf16[8,1024,128]{2,1,0:T(8,128)(2,1)S(1)}, bf16[8,1024,128]{2,1,0:T(8,128)(2,1)}, u32[]{:S(2)}) copy-start(bf16[8,1024,128]{2,1,0:T(8,128)(2,1)} %get-tuple-element.28.slabs_ref) | copy-start | bytes 6291460
  341.9 41.7 %copy-start.3 = (bf16[128,1024]{1,0:T(8,128)(2,1)S(1)}, bf16[128,1024]{1,0:T(8,128)(2,1)}, u32[]{:S(2)}) copy-start(bf16[128,1024]{1,0:T(8,128)(2,1)} %root_ref.9) | copy-start | bytes 786436
  341.9 41.7 %copy-start.5 = (f32[128,1024]{1,0:T(8,128)S(1)}, f32[128,1024]{1,0:T(8,128)}, u32[]{:S(2)}) copy-start(f32[128,1024]{1,0:T(8,128)} %stat_ref.1) | copy-start | bytes 1572868
  400.4 8.5 %copy-start.4 = (bf16[8,512,128]{2,1,0:T(8,128)(2,1)S(1)}, bf16[8,512,128]{2,1,0:T(8,128)(2,1)}, u32[]{:S(2)}) copy-start(bf16[8,512,128]{2,1,0:T(8,128)(2,1)} %get-tuple-element.30.slabs_ref) | copy-start | bytes 3145732
Sparse Core Ops, SparseCore 0:
  10.1 45.1 all-gather.16
  57.4 40.2 all-gather.18
  100.3 47.0 all-gather.10
  149.9 47.1 all-gather.12
  199.6 47.2 all-gather.14
